TPU v7x, 128 devices: a whole 4x4x4 slice. The times are simulated.
128 devices in a mesh: dom: 128 (over x, y, z, core).
Axes of the slice: x: 4, y: 4, z: 4, core: 2. Of those that a mesh axis runs over, the one named last changes fastest.
Arguments:
- positions: float32 [3, 524288], P(None, 'dom'), may hold values from -1.5 to 1.5
- velocity: float32 [3, 524288], P(None, 'dom'), may hold values from -6 to 6
- density_weight: float32 [524288], P('dom'), may hold values from 0.5 to 2
- embed_strength: float32 [524288], P('dom'), may hold values from 0.5 to 2
- occupied: int32 [524288], P('dom'), may hold values 0 or 1
- send_list: int32 [128, 8, 8], P('dom'), may hold values from 0 to 31, as said below
- send_count: int32 [128, 8], P('dom'), may hold values from 0 to 8, as said below
- pair_tiles: int32 [4096, 24], P('dom'), may hold values from 0 to 95, as said below
- pair_count: int32 [4096], P('dom'), may hold values from 1 to 24, as said below
- migrate_dest: int32 [4096], P('dom'), may hold values from 0 to 127, as said below
Outputs:
- force: float32 [3, 524288], P(None, 'dom')
- energy: float32 [524288], P('dom')
- moved: float32 [7, 1048576], P(None, 'dom')
- moved_count: int32 [128], P('dom')
Inputs may be any that keep to these rules, and one draw needn't show every extreme that they name: `send_list`: for one domain and one offset the entries are distinct local tile indices. send_count[s, k] counts the tiles domain s sends to domain s - o_k; it is 0 where that domain does not exist and 8 for some pairs. `pair_tiles`: entries index the frame of the tile's domain; a tile's entries are distinct and its first entry is its own local index. `pair_count`: the first tile of every domain uses all 24 slots. `migrate_dest`: A tile's new domain is within 4 of its domain; at most 4 tiles go from one domain to any other, at most 64 tiles to one domain, and both bounds are reached in every draw.
All inputs are finite; a program needn't handle non-finite values. No bound on the sum of `occupied` on one device may be relied on, other than what follows from the above.
Results may differ from a plain program's by a relative error of at most 0.0003.
Values sent between devices are 32-bit elements; how exact they have to be, the bound alone decides.
A program may use at most 64 MiB of HBM per device.

v0:
```python
import math

import jax
import jax.numpy as jnp
from jax import lax
from jax.sharding import Mesh
from jax.sharding import PartitionSpec as P

TILE = 128
RADIUS = 4
MMAX = 4
DOM = ("dom_0", "dom_1", "dom_2", "dom_3")


CUTOFF_SQUARE = 4.0
REPULSE = 0.05
TIME_STEP = 0.05
EXACT_PRODUCT = lax.Precision.HIGHEST


def shifted(block, axis, distance):
    devices = range(lax.axis_size(axis))
    route = [(i - distance, i) for i in devices if i - distance in devices]
    return lax.ppermute(block, axis, route)


def neutral_like(value, identity):
    return jnp.zeros_like(value) + jnp.asarray(identity, value.dtype)


def entering(value, axes, combine, identity):
    before = start = neutral_like(value, identity)
    running = value
    for axis in reversed(axes):
        size, index = (lax.axis_size(axis), lax.axis_index(axis))
        pieces = lax.all_gather(running, axis)
        inside, running = (start, start)
        for k in range(size):
            passed = k < index
            running = combine(running, pieces[k])
            inside = jnp.where(passed, running, inside)
        before = combine(inside, before)
    return before


def offset_list():
    return [position - RADIUS for position in range(RADIUS)] + [
        position + 1 for position in range(RADIUS)
    ]


def pair_weights(own_occ, near_occ, slot_list, used_count, tile_ids):
    tile_width = own_occ.shape[-1]
    used_mask = (
        jnp.arange(slot_list.shape[1], dtype=jnp.int32)[None, :] < used_count[:, None]
    ).astype(jnp.float32)
    itself = (slot_list == tile_ids[:, None]).astype(jnp.float32)
    identity_mask = jnp.eye(tile_width, dtype=jnp.float32)
    weight = used_mask[:, :, None, None] * own_occ[:, None, :, None] * near_occ[:, :, None, :]
    return weight * (1.0 - itself[:, :, None, None] * identity_mask[None, None])


def closeness(own_pos, near_pos):
    distance = jnp.zeros(near_pos.shape[:2] + (own_pos.shape[2], near_pos.shape[3]), jnp.float32)
    for coordinate in range(3):
        difference = own_pos[:, None, coordinate, :, None] - near_pos[:, :, coordinate, None, :]
        distance = distance + difference * difference
    return jnp.maximum(1.0 - distance / CUTOFF_SQUARE, 0.0)


def density_terms(own_pos, own_occ, near_pos, near_chi, near_occ, slot_list, used_count, tile_ids):
    weight = pair_weights(own_occ, near_occ, slot_list, used_count, tile_ids)
    within = closeness(own_pos, near_pos)
    reach_cube = weight * within * within * within
    density = jnp.sum(reach_cube * near_chi[:, :, None, :], axis=(1, 3))
    pair_energy = jnp.sum(reach_cube * within, axis=(1, 3))
    return (density, pair_energy)


def force_terms(
    own_pos,
    own_occ,
    own_chi,
    own_slope,
    near_pos,
    near_chi,
    near_occ,
    near_slope,
    slot_list,
    used_count,
    tile_ids,
):
    weight = pair_weights(own_occ, near_occ, slot_list, used_count, tile_ids)
    within = closeness(own_pos, near_pos)
    square = within * within
    mixed_slope = (
        own_slope[:, None, :, None] * near_chi[:, :, None, :]
        + near_slope[:, :, None, :] * own_chi[:, None, :, None]
    )
    pair_coef = (
        weight
        * (2.0 / CUTOFF_SQUARE)
        * (3.0 * square * mixed_slope + 4.0 * REPULSE * square * within)
    )
    total_coef = jnp.sum(pair_coef, axis=(1, 3))
    pulled = jnp.einsum("bpij,bpcj->bci", pair_coef, near_pos, precision=EXACT_PRODUCT)
    return own_pos * total_coef[:, None, :] - pulled


def add_counts(earlier, later):
    return earlier + later


def side_places(strides, sign):
    places = [place for place, stride in enumerate(strides) if stride * sign > 0]
    return sorted(places, key=lambda place: abs(strides[place]))


def relay_atoms(blocks, strides):
    result = [None] * len(strides)
    for sign in (1, -1):
        places = side_places(strides, sign)
        pending = jnp.stack([blocks[place] for place in places])
        for place in places:
            pending = shifted(pending, DOM, -sign)
            result[place] = pending[0]
            pending = pending[1:]
    return jnp.stack(result)


def relay_slopes(blocks, strides):
    result = [None] * len(strides)
    for sign in (1, -1):
        places = side_places(strides, sign)
        pending = jnp.stack([blocks[place] for place in places])
        for place in places:
            pending = shifted(pending, DOM, -sign)
            result[place] = pending[0]
            pending = pending[1:]
    return jnp.stack(result)


def per_device(
    positions,
    velocity,
    density_weight,
    embed_strength,
    occupied,
    send_list,
    send_count,
    pair_tiles,
    pair_count,
    migrate_dest,
):
    tile_width = TILE
    tiles_here = pair_tiles.shape[0]
    ghost_most = send_list.shape[2]
    domains = lax.axis_size(DOM)
    own_index = lax.axis_index(DOM)
    strides = offset_list()
    filled = occupied.astype(jnp.float32).reshape(tiles_here, tile_width)
    pos_tiles = positions.reshape(3, tiles_here, tile_width).transpose(1, 0, 2)
    vel_tiles = velocity.reshape(3, tiles_here, tile_width).transpose(1, 0, 2)
    weight_tiles = density_weight.reshape(tiles_here, tile_width)
    embed_tiles = embed_strength.reshape(tiles_here, tile_width)
    packed = jnp.concatenate([pos_tiles, weight_tiles[:, None], filled[:, None]], axis=1)
    live_mask = (jnp.arange(ghost_most, dtype=jnp.int32)[None, :] < send_count[0][:, None]).astype(
        jnp.float32
    )
    blocks = packed[send_list[0]] * live_mask[:, :, None, None]
    ghosts = relay_atoms(blocks, strides)
    frame_tiles = jnp.concatenate([packed, ghosts.reshape(-1, 5, tile_width)], axis=0)
    block_size = math.gcd(tiles_here, 8)
    block_count = tiles_here // block_size
    tile_ids = jnp.arange(tiles_here, dtype=jnp.int32).reshape(block_count, block_size)
    packed_blocks = packed.reshape(block_count, block_size, 5, tile_width)
    slot_blocks = pair_tiles.reshape(block_count, block_size, pair_tiles.shape[1])
    used_blocks = pair_count.reshape(block_count, block_size)

    def density_block(batch_items):
        native, slot_list, used_count, block_ids = batch_items
        nearby = frame_tiles[slot_list]
        return density_terms(
            native[:, 0:3],
            native[:, 4],
            nearby[:, :, 0:3],
            nearby[:, :, 3],
            nearby[:, :, 4],
            slot_list,
            used_count,
            block_ids,
        )

    density, pair_energy = lax.map(
        density_block, (packed_blocks, slot_blocks, used_blocks, tile_ids)
    )
    density = density.reshape(tiles_here, tile_width)
    pair_energy = pair_energy.reshape(tiles_here, tile_width)
    root_term = jnp.sqrt(1.0 + density)
    slope_tiles = -0.5 * embed_tiles * filled / root_term
    energy_tiles = filled * (-embed_tiles * root_term + 0.5 * REPULSE * pair_energy)
    slope_blocks = slope_tiles[send_list[0]] * live_mask[:, :, None]
    ghost_slope = relay_slopes(slope_blocks, strides)
    slope_frame = jnp.concatenate([slope_tiles, ghost_slope.reshape(-1, tile_width)], axis=0)

    def force_block(batch_items):
        native, slot_list, used_count, block_ids, own_slope = batch_items
        nearby = frame_tiles[slot_list]
        near_slope = slope_frame[slot_list]
        return force_terms(
            native[:, 0:3],
            native[:, 4],
            native[:, 3],
            own_slope,
            nearby[:, :, 0:3],
            nearby[:, :, 3],
            nearby[:, :, 4],
            near_slope,
            slot_list,
            used_count,
            block_ids,
        )

    force_tiles = lax.map(
        force_block,
        (
            packed_blocks,
            slot_blocks,
            used_blocks,
            tile_ids,
            slope_tiles.reshape(block_count, block_size, tile_width),
        ),
    )
    force_tiles = force_tiles.reshape(tiles_here, 3, tile_width)
    new_vel = vel_tiles + TIME_STEP * force_tiles
    new_pos = pos_tiles + TIME_STEP * new_vel
    payload = jnp.concatenate([new_pos, new_vel, filled[:, None]], axis=1)
    onehot = (migrate_dest[:, None] == jnp.arange(domains, dtype=jnp.int32)[None, :]).astype(
        jnp.int32
    )
    sent_tiles = jnp.sum(onehot, axis=0)
    rank_within = jnp.sum(onehot * (jnp.cumsum(onehot, axis=0) - onehot), axis=1)
    start_slot = entering(sent_tiles, DOM, add_counts, jnp.zeros_like(sent_tiles))
    capacity = tiles_here + 2 * RADIUS * MMAX
    staying = migrate_dest == own_index
    self_slot = jnp.where(staying, start_slot[own_index] + rank_within, capacity)
    moved_tiles = (
        jnp.zeros((capacity, 7, tile_width), jnp.float32).at[self_slot].set(payload, mode="drop")
    )
    slot_range = jnp.arange(MMAX, dtype=jnp.int32)
    relative = migrate_dest - own_index
    offset_index = jnp.where(relative < 0, relative + RADIUS, relative + RADIUS - 1)
    offset_index = jnp.where(staying, 2 * RADIUS, offset_index)
    outgoing = (
        jnp.zeros((2 * RADIUS, MMAX, 7, tile_width), jnp.float32)
        .at[offset_index, rank_within]
        .set(payload, mode="drop")
    )
    for place, stride in enumerate(strides):
        aim_index = jnp.clip(own_index + stride, 0, domains - 1)
        arrived, their_start, their_sent = shifted(
            (outgoing[place], start_slot[aim_index], sent_tiles[aim_index]), DOM, stride
        )
        slot_list = jnp.where(slot_range < their_sent, their_start + slot_range, capacity)
        moved_tiles = moved_tiles.at[slot_list].set(arrived, mode="drop")
    moved_count = jnp.sum(moved_tiles[:, 6, :]).astype(jnp.int32)[None]
    force = force_tiles.transpose(1, 0, 2).reshape(3, tiles_here * tile_width)
    energy = energy_tiles.reshape(tiles_here * tile_width)
    moved = moved_tiles.transpose(1, 0, 2).reshape(7, capacity * tile_width)
    return (force, energy, moved, moved_count)


def solution(mesh):
    torus = Mesh(mesh.devices.reshape(4, 4, 4, 2), ("dom_0", "dom_1", "dom_2", "dom_3"))
    return jax.shard_map(
        per_device,
        mesh=torus,
        in_specs=(
            P(None, DOM),
            P(None, DOM),
            P(DOM),
            P(DOM),
            P(DOM),
            P(DOM, None, None),
            P(DOM, None),
            P(DOM, None),
            P(DOM),
            P(DOM),
        ),
        out_specs=(P(None, DOM), P(DOM), P(None, DOM), P(DOM)),
        check_vma=False,
    )
```

profile of v0, /device:TPU:2, one launch (start us, length us, event | category | flops | bytes accessed | tf_op | source)
XLA Modules:
  0.0 420.4 jit_solution(8596431277066248943)
XLA Ops:
  6.6 7.9 %collective-permute-start.4 = (f32[4,8,5,128]{3,2,1,0:T(8,128)S(1)}, f32[4,8,5,128]{3,2,1,0:T(8,128)S(1)}, u32[]{:S(2)}, u32[]{:S(2)}) collective-permute-start(f32[4,8,5,128]{3,2,1,0:T(8,128)S(1)} %slice.376), channel_id=1, source_target_pairs={{1,0},{2,1},{3,2},{4,3},{5,4},{6,5},{7,6},{8,7},{9,8},{10,9},{11,1... | collective-permute-start | bytes 245768 | tf_op jit(solution)/shard_map/ppermute | solution.py:24
  16.6 7.0 %all-gather.3 = s32[4,1,128]{2,1,0:T(1,128)S(1)} all-gather(s32[1,1,128]{2,1,0:T(1,128)S(1)} %slice_add_fusion.9), channel_id=3, replica_groups=mesh['dom_0'=4,'dom_1'=4,'dom_2'=4,'dom_3'=2] {'dom_2'}, dimensions={0}, use_global_device_ids=true | all-gather | bytes 2560 | tf_op jit(solution)/shard_map/all_gather | solution.py:36
  23.6 9.8 %all-gather.4 = s32[4,1,128]{2,1,0:T(1,128)S(1)} all-gather(s32[1,1,128]{2,1,0:T(1,128)S(1)} %slice_add_fusion.6), channel_id=1, replica_groups=mesh['dom_0'=4,'dom_1'=4,'dom_2'=4,'dom_3'=2] {'dom_1'}, dimensions={0}, use_global_device_ids=true | all-gather | bytes 2560 | tf_op jit(solution)/shard_map/all_gather | solution.py:36
  33.4 7.8 %all-gather.5 = s32[4,1,128]{2,1,0:T(1,128)S(1)} all-gather(s32[1,1,128]{2,1,0:T(1,128)S(1)} %slice_add_fusion.3), channel_id=1, replica_groups=mesh['dom_0'=4,'dom_1'=4,'dom_2'=4,'dom_3'=2] {'dom_0'}, dimensions={0}, use_global_device_ids=true | all-gather | bytes 2560 | tf_op jit(solution)/shard_map/all_gather | solution.py:36
  58.1 6.9 %collective-permute-done.1 = f32[3,8,5,128]{3,2,1,0:T(8,128)S(1)} collective-permute-done((f32[3,8,5,128]{3,2,1,0:T(8,128)S(1)}, f32[3,8,5,128]{3,2,1,0:T(8,128)S(1)}, u32[]{:S(2)}, u32[]{:S(2)}) %collective-permute-start.1) | collective-permute-done | bytes 61472 | tf_op jit(solution)/shard_map/ppermute | solution.py:24
  88.7 7.4 %collective-permute-start.25 = (s32[]{:T(128)}, s32[]{:T(128)}, u32[]{:S(2)}, u32[]{:S(2)}) collective-permute-start(s32[]{:T(128)} %bitcast.87), channel_id=1, source_target_pairs={{1,0},{2,1},{3,2},{4,3},{5,4},{6,5},{7,6},{8,7},{9,8},{10,9},{11,1... | collective-permute-start | bytes 20 | tf_op jit(solution)/shard_map/ppermute | solution.py:24
  103.8 7.9 %collective-permute-start.7 = (f32[1,8,5,128]{3,2,1,0:T(8,128)S(1)}, f32[1,8,5,128]{3,2,1,0:T(8,128)S(1)}, u32[]{:S(2)}, u32[]{:S(2)}) collective-permute-start(f32[1,8,5,128]{3,2,1,0:T(8,128)S(1)} %get-tuple-element.180), channel_id=1, source_target_pairs={{1,0},{2,1},{3,2},{4,3},{5,4},{6,5},{7,6},{8,7},{9,8},{10,9},{11,1... | collective-permute-start | bytes 61448 | tf_op jit(solution)/shard_map/ppermute | solution.py:24
  115.5 51.5 %while.22 = (s32[]{:T(128)}, f32[4,8,128]{2,1,0:T(8,128)S(1)}, f32[4,8,128]{2,1,0:T(8,128)S(1)}, s32[4,8]{1,0:T(4,128)S(1)}, f32[4,8,5,128]{3,1,2,0:T(8,128)S(1)...) while((s32[]{:T(128)}, f32[4,8,128]{2,1,0:T(8,128)S(1)}, ...), condition=%wide.region_3.4_spmd, body=%wide.region_0.3_spmd.sunk | while | flops 69263680 | bytes 2912821 | solution.py:194
  117.2 11.1 %multiply_reduce_fusion.3 = (f32[8,128]{1,0:T(8,128)S(1)}, f32[8,128]{1,0:T(8,128)S(1)}) fusion(f32[8,24,128]{2,1,0:T(8,128)S(1)} %bitcast.284, f32[8,128]{1,0:T(8,128)S(1)} %get-tuple-element.326, f32[8,24,128]{2,1,0:T(8,128)S(1)} %bitcast.285, f32[8,128]{1,0:T(8,128)S(1)} %get-tuple-element.328, f32[8,24,128]{2,1,0:T(8,128)S(1)} %bitcast.286, ...), kind=kLoop, calls=%fused_computation.16.clone.1 | loop fusion | flops 69203968 | bytes 676608 | tf_op jit(solution)/shard_map/while/body/eval_jaxpr/reduce_sum | solution.py:76
  130.1 11.1 %multiply_reduce_fusion.3 = (f32[8,128]{1,0:T(8,128)S(1)}, f32[8,128]{1,0:T(8,128)S(1)}) fusion(f32[8,24,128]{2,1,0:T(8,128)S(1)} %bitcast.284, f32[8,128]{1,0:T(8,128)S(1)} %get-tuple-element.326, f32[8,24,128]{2,1,0:T(8,128)S(1)} %bitcast.285, f32[8,128]{1,0:T(8,128)S(1)} %get-tuple-element.328, f32[8,24,128]{2,1,0:T(8,128)S(1)} %bitcast.286, ...), kind=kLoop, calls=%fused_computation.16.clone.1 | loop fusion | flops 69203968 | bytes 676608 | tf_op jit(solution)/shard_map/while/body/eval_jaxpr/reduce_sum | solution.py:76
  143.0 11.1 %multiply_reduce_fusion.3 = (f32[8,128]{1,0:T(8,128)S(1)}, f32[8,128]{1,0:T(8,128)S(1)}) fusion(f32[8,24,128]{2,1,0:T(8,128)S(1)} %bitcast.284, f32[8,128]{1,0:T(8,128)S(1)} %get-tuple-element.326, f32[8,24,128]{2,1,0:T(8,128)S(1)} %bitcast.285, f32[8,128]{1,0:T(8,128)S(1)} %get-tuple-element.328, f32[8,24,128]{2,1,0:T(8,128)S(1)} %bitcast.286, ...), kind=kLoop, calls=%fused_computation.16.clone.1 | loop fusion | flops 69203968 | bytes 676608 | tf_op jit(solution)/shard_map/while/body/eval_jaxpr/reduce_sum | solution.py:76
  155.8 11.1 %multiply_reduce_fusion.3 = (f32[8,128]{1,0:T(8,128)S(1)}, f32[8,128]{1,0:T(8,128)S(1)}) fusion(f32[8,24,128]{2,1,0:T(8,128)S(1)} %bitcast.284, f32[8,128]{1,0:T(8,128)S(1)} %get-tuple-element.326, f32[8,24,128]{2,1,0:T(8,128)S(1)} %bitcast.285, f32[8,128]{1,0:T(8,128)S(1)} %get-tuple-element.328, f32[8,24,128]{2,1,0:T(8,128)S(1)} %bitcast.286, ...), kind=kLoop, calls=%fused_computation.16.clone.1 | loop fusion | flops 69203968 | bytes 676608 | tf_op jit(solution)/shard_map/while/body/eval_jaxpr/reduce_sum | solution.py:76
  213.8 7.8 %collective-permute-start.14 = (f32[2,8,128]{2,1,0:T(8,128)S(1)}, f32[2,8,128]{2,1,0:T(8,128)S(1)}, u32[]{:S(2)}, u32[]{:S(2)}) collective-permute-start(f32[2,8,128]{2,1,0:T(8,128)S(1)} %slice.397), channel_id=1, source_target_pairs={{1,0},{2,1},{3,2},{4,3},{5,4},{6,5},{7,6},{8,7},{9,8},{10,9},{11,1... | collective-permute-start | bytes 24584 | tf_op jit(solution)/shard_map/ppermute | solution.py:24
  223.0 8.0 %collective-permute-start.15 = (f32[1,8,128]{2,1,0:T(8,128)S(1)}, f32[1,8,128]{2,1,0:T(8,128)S(1)}, u32[]{:S(2)}, u32[]{:S(2)}) collective-permute-start(f32[1,8,128]{2,1,0:T(8,128)S(1)} %get-tuple-element.186), channel_id=1, source_target_pairs={{1,0},{2,1},{3,2},{4,3},{5,4},{6,5},{7,6},{8,7},{9,8},{10,9},{11,1... | collective-permute-start | bytes 12296 | tf_op jit(solution)/shard_map/ppermute | solution.py:24
  232.2 144.7 %while.23 = (s32[]{:T(128)}, f32[4,8,3,128]{3,2,1,0:T(4,128)S(1)}, f32[4,8,5,128]{3,2,1,0:T(8,128)S(1)}, s32[4,8]{1,0:T(4,128)S(1)}, s32[4,8,24]{2,1,0:T(8,128)S...) while((s32[]{:T(128)}, f32[4,8,3,128]{3,2,1,0:T(4,128)S(1)}, ...), condition=%wide.region_6.7_spmd, body=%wide.region_4.6_spmd.sunk | while | flops 280034624 | bytes 4420925 | solution.py:224
  234.6 13.2 %fusion.78 = f32[8,128]{1,0:T(8,128)S(1)} fusion(f32[8,128]{1,0:T(8,128)S(1)} %bitcast.294, f32[8,24,128]{2,1,0:T(8,128)S(1)} %bitcast.271, f32[8,24,128]{2,1,0:T(8,128)S(1)} %bitcast.275, f32[8,128]{1,0:T(8,128)S(1)} %dynamic-slice_bitcast_fusion.8, f32[8,24,128]{2,1,0:T(8,128)S(1)} %bitcast.277, f32[8,128]{1,0:T(8,128)S(1)} %bitcast.296, ...), kind=kLoop, calls=%fused_computation.41.clone.1 | loop fusion | flops 84933632 | bytes 779008 | tf_op jit(solution)/shard_map/while/body/eval_jaxpr/reduce_sum | solution.py:105
  247.8 20.5 %fusion.79 = f32[4,8,3,128]{3,2,1,0:T(4,128)S(1)} fusion(f32[4,8,3,128]{3,2,1,0:T(4,128)S(1)} %get-tuple-element.397, s32[]{:T(128)} %get-tuple-element.396, f32[8,128]{1,0:T(8,128)S(1)} %bitcast.295, f32[8,24,128]{2,1,0:T(8,128)S(1)} %bitcast.272, f32[8,24,128]{2,1,0:T(8,128)S(1)} %bitcast.276, f32[8,128]{1,0:T(8,128)S(1)} %dynamic-slice_bitcast_fusion.8, ...), kind=kOutput, calls=%fused_computation.45.clone.1 | convolution fusion | flops 195041280 | bytes 1208324 | tf_op jit(solution)/shard_map/while/body/eval_jaxpr/bpij,bpcj->bci/dot_general | solution.py:106
  270.7 13.2 %fusion.78 = f32[8,128]{1,0:T(8,128)S(1)} fusion(f32[8,128]{1,0:T(8,128)S(1)} %bitcast.294, f32[8,24,128]{2,1,0:T(8,128)S(1)} %bitcast.271, f32[8,24,128]{2,1,0:T(8,128)S(1)} %bitcast.275, f32[8,128]{1,0:T(8,128)S(1)} %dynamic-slice_bitcast_fusion.8, f32[8,24,128]{2,1,0:T(8,128)S(1)} %bitcast.277, f32[8,128]{1,0:T(8,128)S(1)} %bitcast.296, ...), kind=kLoop, calls=%fused_computation.41.clone.1 | loop fusion | flops 84933632 | bytes 779008 | tf_op jit(solution)/shard_map/while/body/eval_jaxpr/reduce_sum | solution.py:105
  283.9 20.5 %fusion.79 = f32[4,8,3,128]{3,2,1,0:T(4,128)S(1)} fusion(f32[4,8,3,128]{3,2,1,0:T(4,128)S(1)} %get-tuple-element.397, s32[]{:T(128)} %get-tuple-element.396, f32[8,128]{1,0:T(8,128)S(1)} %bitcast.295, f32[8,24,128]{2,1,0:T(8,128)S(1)} %bitcast.272, f32[8,24,128]{2,1,0:T(8,128)S(1)} %bitcast.276, f32[8,128]{1,0:T(8,128)S(1)} %dynamic-slice_bitcast_fusion.8, ...), kind=kOutput, calls=%fused_computation.45.clone.1 | convolution fusion | flops 195041280 | bytes 1208324 | tf_op jit(solution)/shard_map/while/body/eval_jaxpr/bpij,bpcj->bci/dot_general | solution.py:106
  306.8 13.2 %fusion.78 = f32[8,128]{1,0:T(8,128)S(1)} fusion(f32[8,128]{1,0:T(8,128)S(1)} %bitcast.294, f32[8,24,128]{2,1,0:T(8,128)S(1)} %bitcast.271, f32[8,24,128]{2,1,0:T(8,128)S(1)} %bitcast.275, f32[8,128]{1,0:T(8,128)S(1)} %dynamic-slice_bitcast_fusion.8, f32[8,24,128]{2,1,0:T(8,128)S(1)} %bitcast.277, f32[8,128]{1,0:T(8,128)S(1)} %bitcast.296, ...), kind=kLoop, calls=%fused_computation.41.clone.1 | loop fusion | flops 84933632 | bytes 779008 | tf_op jit(solution)/shard_map/while/body/eval_jaxpr/reduce_sum | solution.py:105
  320.0 20.5 %fusion.79 = f32[4,8,3,128]{3,2,1,0:T(4,128)S(1)} fusion(f32[4,8,3,128]{3,2,1,0:T(4,128)S(1)} %get-tuple-element.397, s32[]{:T(128)} %get-tuple-element.396, f32[8,128]{1,0:T(8,128)S(1)} %bitcast.295, f32[8,24,128]{2,1,0:T(8,128)S(1)} %bitcast.272, f32[8,24,128]{2,1,0:T(8,128)S(1)} %bitcast.276, f32[8,128]{1,0:T(8,128)S(1)} %dynamic-slice_bitcast_fusion.8, ...), kind=kOutput, calls=%fused_computation.45.clone.1 | convolution fusion | flops 195041280 | bytes 1208324 | tf_op jit(solution)/shard_map/while/body/eval_jaxpr/bpij,bpcj->bci/dot_general | solution.py:106
  343.0 13.2 %fusion.78 = f32[8,128]{1,0:T(8,128)S(1)} fusion(f32[8,128]{1,0:T(8,128)S(1)} %bitcast.294, f32[8,24,128]{2,1,0:T(8,128)S(1)} %bitcast.271, f32[8,24,128]{2,1,0:T(8,128)S(1)} %bitcast.275, f32[8,128]{1,0:T(8,128)S(1)} %dynamic-slice_bitcast_fusion.8, f32[8,24,128]{2,1,0:T(8,128)S(1)} %bitcast.277, f32[8,128]{1,0:T(8,128)S(1)} %bitcast.296, ...), kind=kLoop, calls=%fused_computation.41.clone.1 | loop fusion | flops 84933632 | bytes 779008 | tf_op jit(solution)/shard_map/while/body/eval_jaxpr/reduce_sum | solution.py:105
  356.2 20.5 %fusion.79 = f32[4,8,3,128]{3,2,1,0:T(4,128)S(1)} fusion(f32[4,8,3,128]{3,2,1,0:T(4,128)S(1)} %get-tuple-element.397, s32[]{:T(128)} %get-tuple-element.396, f32[8,128]{1,0:T(8,128)S(1)} %bitcast.295, f32[8,24,128]{2,1,0:T(8,128)S(1)} %bitcast.272, f32[8,24,128]{2,1,0:T(8,128)S(1)} %bitcast.276, f32[8,128]{1,0:T(8,128)S(1)} %dynamic-slice_bitcast_fusion.8, ...), kind=kOutput, calls=%fused_computation.45.clone.1 | convolution fusion | flops 195041280 | bytes 1208324 | tf_op jit(solution)/shard_map/while/body/eval_jaxpr/bpij,bpcj->bci/dot_general | solution.py:106
  383.0 7.7 %collective-permute-start.24 = (f32[4,7,128]{2,1,0:T(8,128)S(1)}, f32[4,7,128]{2,1,0:T(8,128)S(1)}, u32[]{:S(2)}, u32[]{:S(2)}) collective-permute-start(f32[4,7,128]{2,1,0:T(8,128)S(1)} %get-tuple-element.177), channel_id=1, source_target_pairs={{2,0},{3,1},{4,2},{5,3},{6,4},{7,5},{8,6},{9,7},{10,8},{11,9},{12,... | collective-permute-start | bytes 43016 | tf_op jit(solution)/shard_map/ppermute | solution.py:24
  (332 shorter events, 158.0 us)
Async XLA Ops:
  4.7 50.2 %collective-permute-start = (f32[4,8,5,128]{3,2,1,0:T(8,128)S(1)}, f32[4,8,5,128]{3,2,1,0:T(8,128)S(1)}, u32[]{:S(2)}, u32[]{:S(2)}) collective-permute-start(f32[4,8,5,128]{3,2,1,0:T(8,128)S(1)} %pad_maximum_fusion.3), channel_id=1, source_target_pairs={{0,1},{1,2},{2,3},{3,4},{4,5},{5,6},{6,7},{7,8},{8,9},{9,10},{10,1... | collective-permute-start | bytes 245768 | tf_op jit(solution)/shard_map/ppermute | solution.py:24
  6.6 66.1 %collective-permute-start.4 = (f32[4,8,5,128]{3,2,1,0:T(8,128)S(1)}, f32[4,8,5,128]{3,2,1,0:T(8,128)S(1)}, u32[]{:S(2)}, u32[]{:S(2)}) collective-permute-start(f32[4,8,5,128]{3,2,1,0:T(8,128)S(1)} %slice.376), channel_id=1, source_target_pairs={{1,0},{2,1},{3,2},{4,3},{5,4},{6,5},{7,6},{8,7},{9,8},{10,9},{11,1... | collective-permute-start | bytes 245768 | tf_op jit(solution)/shard_map/ppermute | solution.py:24
  41.9 25.0 %collective-permute-start.17 = (s32[]{:T(128)}, s32[]{:T(128)}, u32[]{:S(2)}, u32[]{:S(2)}) collective-permute-start(s32[]{:T(128)} %bitcast.73), channel_id=1, source_target_pairs={{4,0},{5,1},{6,2},{7,3},{8,4},{9,5},{10,6},{11,7},{12,8},{13,9},{1... | collective-permute-start | bytes 20 | tf_op jit(solution)/shard_map/ppermute | solution.py:24
  46.5 22.4 %collective-permute-start.16 = (s32[]{:T(128)}, s32[]{:T(128)}, u32[]{:S(2)}, u32[]{:S(2)}) collective-permute-start(s32[]{:T(128)} %bitcast.72), channel_id=1, source_target_pairs={{4,0},{5,1},{6,2},{7,3},{8,4},{9,5},{10,6},{11,7},{12,8},{13,9},{1... | collective-permute-start | bytes 20 | tf_op jit(solution)/shard_map/ppermute | solution.py:24
  51.0 31.6 %collective-permute-start.20 = (s32[]{:T(128)}, s32[]{:T(128)}, u32[]{:S(2)}, u32[]{:S(2)}) collective-permute-start(s32[]{:T(128)} %bitcast.80), channel_id=1, source_target_pairs={{3,0},{4,1},{5,2},{6,3},{7,4},{8,5},{9,6},{10,7},{11,8},{12,9},{13... | collective-permute-start | bytes 20 | tf_op jit(solution)/shard_map/ppermute | solution.py:24
  65.0 19.5 %collective-permute-start.19 = (s32[]{:T(128)}, s32[]{:T(128)}, u32[]{:S(2)}, u32[]{:S(2)}) collective-permute-start(s32[]{:T(128)} %bitcast.79), channel_id=1, source_target_pairs={{3,0},{4,1},{5,2},{6,3},{7,4},{8,5},{9,6},{10,7},{11,8},{12,9},{13... | collective-permute-start | bytes 20 | tf_op jit(solution)/shard_map/ppermute | solution.py:24
  67.0 34.8 %collective-permute-start.23 = (s32[]{:T(128)}, s32[]{:T(128)}, u32[]{:S(2)}, u32[]{:S(2)}) collective-permute-start(s32[]{:T(128)} %bitcast.84), channel_id=1, source_target_pairs={{2,0},{3,1},{4,2},{5,3},{6,4},{7,5},{8,6},{9,7},{10,8},{11,9},{12,... | collective-permute-start | bytes 20 | tf_op jit(solution)/shard_map/ppermute | solution.py:24
  72.7 31.0 %collective-permute-start.22 = (s32[]{:T(128)}, s32[]{:T(128)}, u32[]{:S(2)}, u32[]{:S(2)}) collective-permute-start(s32[]{:T(128)} %bitcast.83), channel_id=1, source_target_pairs={{2,0},{3,1},{4,2},{5,3},{6,4},{7,5},{8,6},{9,7},{10,8},{11,9},{12,... | collective-permute-start | bytes 20 | tf_op jit(solution)/shard_map/ppermute | solution.py:24
  78.7 89.1 %collective-permute-start.26 = (s32[]{:T(128)}, s32[]{:T(128)}, u32[]{:S(2)}, u32[]{:S(2)}) collective-permute-start(s32[]{:T(128)} %bitcast.88), channel_id=1, source_target_pairs={{1,0},{2,1},{3,2},{4,3},{5,4},{6,5},{7,6},{8,7},{9,8},{10,9},{11,1... | collective-permute-start | bytes 20 | tf_op jit(solution)/shard_map/ppermute | solution.py:24
  88.7 81.0 %collective-permute-start.25 = (s32[]{:T(128)}, s32[]{:T(128)}, u32[]{:S(2)}, u32[]{:S(2)}) collective-permute-start(s32[]{:T(128)} %bitcast.87), channel_id=1, source_target_pairs={{1,0},{2,1},{3,2},{4,3},{5,4},{6,5},{7,6},{8,7},{9,8},{10,9},{11,1... | collective-permute-start | bytes 20 | tf_op jit(solution)/shard_map/ppermute | solution.py:24
  99.9 81.1 %collective-permute-start.29 = (s32[]{:T(128)}, s32[]{:T(128)}, u32[]{:S(2)}, u32[]{:S(2)}) collective-permute-start(s32[]{:T(128)} %bitcast.92), channel_id=1, source_target_pairs={{0,1},{1,2},{2,3},{3,4},{4,5},{5,6},{6,7},{7,8},{8,9},{9,10},{10,1... | collective-permute-start | bytes 20 | tf_op jit(solution)/shard_map/ppermute | solution.py:24
  101.8 81.1 %collective-permute-start.28 = (s32[]{:T(128)}, s32[]{:T(128)}, u32[]{:S(2)}, u32[]{:S(2)}) collective-permute-start(s32[]{:T(128)} %bitcast.91), channel_id=1, source_target_pairs={{0,1},{1,2},{2,3},{3,4},{4,5},{5,6},{6,7},{7,8},{8,9},{9,10},{10,1... | collective-permute-start | bytes 20 | tf_op jit(solution)/shard_map/ppermute | solution.py:24
  113.5 80.6 %collective-permute-start.32 = (s32[]{:T(128)}, s32[]{:T(128)}, u32[]{:S(2)}, u32[]{:S(2)}) collective-permute-start(s32[]{:T(128)} %bitcast.96), channel_id=1, source_target_pairs={{0,2},{1,3},{2,4},{3,5},{4,6},{5,7},{6,8},{7,9},{8,10},{9,11},{10,... | collective-permute-start | bytes 20 | tf_op jit(solution)/shard_map/ppermute | solution.py:24
  167.8 28.7 %collective-permute-start.31 = (s32[]{:T(128)}, s32[]{:T(128)}, u32[]{:S(2)}, u32[]{:S(2)}) collective-permute-start(s32[]{:T(128)} %bitcast.95), channel_id=1, source_target_pairs={{0,2},{1,3},{2,4},{3,5},{4,6},{5,7},{6,8},{7,9},{8,10},{9,11},{10,... | collective-permute-start | bytes 20 | tf_op jit(solution)/shard_map/ppermute | solution.py:24
  179.0 31.0 %collective-permute-start.35 = (s32[]{:T(128)}, s32[]{:T(128)}, u32[]{:S(2)}, u32[]{:S(2)}) collective-permute-start(s32[]{:T(128)} %bitcast.100), channel_id=1, source_target_pairs={{0,3},{1,4},{2,5},{3,6},{4,7},{5,8},{6,9},{7,10},{8,11},{9,12},{10... | collective-permute-start | bytes 20 | tf_op jit(solution)/shard_map/ppermute | solution.py:24
  180.9 31.0 %collective-permute-start.34 = (s32[]{:T(128)}, s32[]{:T(128)}, u32[]{:S(2)}, u32[]{:S(2)}) collective-permute-start(s32[]{:T(128)} %bitcast.99), channel_id=1, source_target_pairs={{0,3},{1,4},{2,5},{3,6},{4,7},{5,8},{6,9},{7,10},{8,11},{9,12},{10... | collective-permute-start | bytes 20 | tf_op jit(solution)/shard_map/ppermute | solution.py:24
  192.1 198.6 %collective-permute-start.38 = (s32[]{:T(128)}, s32[]{:T(128)}, u32[]{:S(2)}, u32[]{:S(2)}) collective-permute-start(s32[]{:T(128)} %bitcast.104), channel_id=1, source_target_pairs={{0,4},{1,5},{2,6},{3,7},{4,8},{5,9},{6,10},{7,11},{8,12},{9,13},{1... | collective-permute-start | bytes 20 | tf_op jit(solution)/shard_map/ppermute | solution.py:24
  200.2 190.5 %collective-permute-start.37 = (s32[]{:T(128)}, s32[]{:T(128)}, u32[]{:S(2)}, u32[]{:S(2)}) collective-permute-start(s32[]{:T(128)} %bitcast.103), channel_id=1, source_target_pairs={{0,4},{1,5},{2,6},{3,7},{4,8},{5,9},{6,10},{7,11},{8,12},{9,13},{1... | collective-permute-start | bytes 20 | tf_op jit(solution)/shard_map/ppermute | solution.py:24
  379.1 17.3 %collective-permute-start.18 = (f32[4,7,128]{2,1,0:T(8,128)S(1)}, f32[4,7,128]{2,1,0:T(8,128)S(1)}, u32[]{:S(2)}, u32[]{:S(2)}) collective-permute-start(f32[4,7,128]{2,1,0:T(8,128)S(1)} %get-tuple-element.179), channel_id=1, source_target_pairs={{4,0},{5,1},{6,2},{7,3},{8,4},{9,5},{10,6},{11,7},{12,8},{13,9},{1... | collective-permute-start | bytes 43016 | tf_op jit(solution)/shard_map/ppermute | solution.py:24
  381.0 18.6 %collective-permute-start.21 = (f32[4,7,128]{2,1,0:T(8,128)S(1)}, f32[4,7,128]{2,1,0:T(8,128)S(1)}, u32[]{:S(2)}, u32[]{:S(2)}) collective-permute-start(f32[4,7,128]{2,1,0:T(8,128)S(1)} %get-tuple-element.178), channel_id=1, source_target_pairs={{3,0},{4,1},{5,2},{6,3},{7,4},{8,5},{9,6},{10,7},{11,8},{12,9},{13... | collective-permute-start | bytes 43016 | tf_op jit(solution)/shard_map/ppermute | solution.py:24
  383.0 20.9 %collective-permute-start.24 = (f32[4,7,128]{2,1,0:T(8,128)S(1)}, f32[4,7,128]{2,1,0:T(8,128)S(1)}, u32[]{:S(2)}, u32[]{:S(2)}) collective-permute-start(f32[4,7,128]{2,1,0:T(8,128)S(1)} %get-tuple-element.177), channel_id=1, source_target_pairs={{2,0},{3,1},{4,2},{5,3},{6,4},{7,5},{8,6},{9,7},{10,8},{11,9},{12,... | collective-permute-start | bytes 43016 | tf_op jit(solution)/shard_map/ppermute | solution.py:24
  392.0 22.5 %collective-permute-start.27 = (f32[4,7,128]{2,1,0:T(8,128)S(1)}, f32[4,7,128]{2,1,0:T(8,128)S(1)}, u32[]{:S(2)}, u32[]{:S(2)}) collective-permute-start(f32[4,7,128]{2,1,0:T(8,128)S(1)} %get-tuple-element.176), channel_id=1, source_target_pairs={{1,0},{2,1},{3,2},{4,3},{5,4},{6,5},{7,6},{8,7},{9,8},{10,9},{11,1... | collective-permute-start | bytes 43016 | tf_op jit(solution)/shard_map/ppermute | solution.py:24
  394.0 21.2 %collective-permute-start.30 = (f32[4,7,128]{2,1,0:T(8,128)S(1)}, f32[4,7,128]{2,1,0:T(8,128)S(1)}, u32[]{:S(2)}, u32[]{:S(2)}) collective-permute-start(f32[4,7,128]{2,1,0:T(8,128)S(1)} %get-tuple-element.175), channel_id=1, source_target_pairs={{0,1},{1,2},{2,3},{3,4},{4,5},{5,6},{6,7},{7,8},{8,9},{9,10},{10,1... | collective-permute-start | bytes 43016 | tf_op jit(solution)/shard_map/ppermute | solution.py:24
  396.4 19.4 %collective-permute-start.33 = (f32[4,7,128]{2,1,0:T(8,128)S(1)}, f32[4,7,128]{2,1,0:T(8,128)S(1)}, u32[]{:S(2)}, u32[]{:S(2)}) collective-permute-start(f32[4,7,128]{2,1,0:T(8,128)S(1)} %get-tuple-element.174), channel_id=1, source_target_pairs={{0,2},{1,3},{2,4},{3,5},{4,6},{5,7},{6,8},{7,9},{8,10},{9,11},{10,... | collective-permute-start | bytes 43016 | tf_op jit(solution)/shard_map/ppermute | solution.py:24
  (44 other events, 1756.2 us)
where the time goes:
time: 422 us; the launch traced here: 420 us
  starting transfers between devices  133 us (32%)
  other arithmetic  120 us (28%)
  matrix products  82.1 us (19%)
  waiting for transfers between devices  28.3 us (7%)
  blocking collectives  26.4 us (6%)
  local copies, waits for them, and re-layouts  25.5 us (6%)
    ppermute x40, starting transfers between devices, shifted(): return lax.ppermute(block, axis, route)  133 us
    dot_general x4, matrix products, force_terms(): jnp.einsum('bpij,bpcj->bci', pair_coef, near_pos, precision=EXACT_PRODUCT)  82.1 us
    reduce_sum x4, other arithmetic, force_terms(): total_coef = jnp.sum(pair_coef, axis=(1, 3))  52.8 us
    reduce_sum x4, other arithmetic, density_terms(): pair_energy = jnp.sum(reach_cube * within, axis=(1, 3))  44.6 us
    ppermute x40, waiting for transfers between devices, shifted(): return lax.ppermute(block, axis, route)  28.3 us
    all_gather x4, blocking collectives, entering(): pieces = lax.all_gather(running, axis)  26.4 us
    select_n x8, other arithmetic, per_device(): moved_tiles = moved_tiles.at[slot_list].set(arrived, mode='drop')  13.9 us
  transfers between devices with their start and end apart: 40, of which 8 were waited for; matrix products, arithmetic and copies ran while one was open for 53% of the time, Pallas kernels for 0%

commit v1 on v0

v1 whole, which is shorter than its diff:
```python
import functools

import jax
import jax.numpy as jnp
from jax import lax
from jax.experimental import pallas as pl
from jax.experimental.pallas import tpu as pltpu
from jax.sharding import PartitionSpec as P

MESH = pl.DeviceIdType.MESH
VMEM = pltpu.VMEM
SMEM = pltpu.SMEM
F32 = jnp.float32
BF16 = jnp.bfloat16
I32 = jnp.int32
KEPT = VMEM

OFFSETS = (-4, -3, -2, -1, 1, 2, 3, 4)
WIDE = 128
OWN = 32
GHOST = 64
FRAME = OWN + GHOST
PAIRS = 24
CAP = 64
HAND = 4
FEAT = 32
ROWS = 24
UNITS = 16
LIST = OWN * PAIRS // 2 + PAIRS // 2 + UNITS
STEP = 0.05
EMPTY = 64.0


def round_bf16(value):
    return value.astype(BF16).astype(F32)


def two_parts(value):
    high = round_bf16(value)
    return high, round_bf16(value - high)


def three_parts(value):
    high, middle = two_parts(value)
    return high, middle, round_bf16(value - high - middle)


def peer(shift):
    size = lax.axis_size("dom")
    return (lax.rem(lax.axis_index("dom") + shift + size, size),)


def greet():
    barrier = pltpu.get_barrier_semaphore()
    for shift in OFFSETS:
        pl.semaphore_signal(barrier, inc=1, device_id=peer(shift), device_id_type=MESH)
    return barrier


def send_block(src, dst, send_sem, recv_sem, shift):
    copy = pltpu.make_async_remote_copy(
        src_ref=src,
        dst_ref=dst,
        send_sem=send_sem,
        recv_sem=recv_sem,
        device_id=peer(shift),
        device_id_type=MESH,
    )
    copy.start()
    return copy


def every(start, step):
    return pl.ds(start, 8, stride=step)


def atoms_kernel(
    pos, vel, chi, occ, slist, scount, pack, ghost, send, land, send_sem, recv_sem
):
    barrier = greet()
    flat = pack.reshape(OWN * 8, WIDE)
    for tile in range(OWN):
        columns = pl.ds(tile * WIDE, WIDE)
        flat[pl.ds(tile * 8, 3), :] = pos[:, columns]
        flat[pl.ds(tile * 8 + 3, 3), :] = vel[:, columns]
    for group in range(OWN // 8):
        rows = pl.ds(group * 8, 8)
        flat[every(group * 64 + 6, 8), :] = occ[rows, :].astype(F32)
        flat[every(group * 64 + 7, 8), :] = chi[rows, :]
    slots = lax.broadcasted_iota(I32, (8, WIDE), 0)
    used = scount[...]
    for place in range(8):
        for slot in range(8):
            held = pack[slist[0, place, slot]]
            send[place, pl.ds(slot, 3, stride=8), :] = held[0:3]
            send[place, pl.ds(24 + slot, 1), :] = held[6:7]
            send[place, pl.ds(32 + slot, 1), :] = held[7:8]
        live = jnp.broadcast_to(used[:, place : place + 1], (8, WIDE)) > slots
        filled = send[place, pl.ds(24, 8), :]
        send[place, pl.ds(24, 8), :] = jnp.where(live, filled, 0.0)
    pl.semaphore_wait(barrier, len(OFFSETS))
    copies = [
        send_block(send.at[p], land.at[p], send_sem.at[p], recv_sem.at[p], -shift)
        for p, shift in enumerate(OFFSETS)
    ]
    for copy in copies:
        copy.wait()
    for place in range(8):
        ghost[place] = land[place]


def fields(group, pack, ghost):
    if group < OWN // 8:
        return [pack[every(group * 64 + row, 8), :] for row in (0, 1, 2, 6, 7)]
    return [ghost[group - OWN // 8, pl.ds(row * 8, 8), :] for row in range(5)]


def place_factors(group, pack, ghost):
    x, y, z, filled, chi = fields(group, pack, ghost)
    parts = [two_parts(0.5 * value) for value in (x, y, z)]
    high = [part[0] for part in parts]
    low = [part[1] for part in parts]
    whole = [h + l for h, l in parts]
    norm = whole[0] * whole[0] + whole[1] * whole[1] + whole[2] * whole[2]
    return high, low, whole, norm, filled, chi


def near_rows(high, low, norm, filled):
    one = jnp.ones_like(norm)
    reach_norm = three_parts(-norm - EMPTY * (1.0 - filled))
    return high + low + high + low + list(reach_norm) + [one, one, one]


def own_rows(high, low, norm):
    one = jnp.ones_like(norm)
    twice_high = [2.0 * h for h in high]
    twice_low = [2.0 * l for l in low]
    rows = twice_high + twice_high + twice_low + twice_low
    return rows + [one, one, one] + list(three_parts(1.0 - norm))


def put_rows(ref, group, rows):
    for k, row in enumerate(rows):
        ref[every(group * 8 * len(rows) + k, len(rows)), :] = row


def padded(ref, tile):
    rows = ref[pl.ds(pl.multiple_of(tile * ROWS, 8), ROWS), :]
    return jnp.concatenate([rows, jnp.zeros((FEAT - ROWS, WIDE), F32)], axis=0)


def total_rows(ref):
    return jnp.sum(ref.T, axis=0, keepdims=True)


def density_kernel(
    pack, ghost, embed, pair_tiles, pair_count, dest,
    slope, energy, near, units, trips, slots, counts,
    own_raw, near_raw, own, chis, acc,
):
    pack = pack.reshape(OWN * 8, WIDE)
    zero = jnp.zeros((8, WIDE), F32)
    blank = [zero] * (ROWS - 18)
    for group in range(FRAME // 8):
        high, low, whole, norm, filled, chi = place_factors(group, pack, ghost)
        put_rows(near_raw, group, near_rows(high, low, norm, filled) + blank)
        chis[pl.ds(group * 8, 8), :] = chi
        if group < OWN // 8:
            put_rows(own_raw, group, own_rows(high, low, norm) + blank)
    chis[pl.ds(FRAME, 8), :] = zero
    near[FRAME] = jnp.zeros((FEAT, WIDE), BF16)

    def near_step(tile, carry):
        near[tile] = padded(near_raw, tile).astype(BF16)
        return carry

    lax.fori_loop(0, FRAME, near_step, 0, unroll=8)

    def own_step(tile, carry):
        own[tile] = padded(own_raw, tile).T.astype(BF16)
        for k in range(2):
            acc[k, tile] = jnp.zeros((WIDE, WIDE), F32)
        return carry

    lax.fori_loop(0, OWN, own_step, 0, unroll=4)
    own[OWN] = jnp.zeros((WIDE, FEAT), BF16)

    def list_step(tile, base):
        used = pair_count[tile]
        for k in range(PAIRS // 2):
            first = pair_tiles[2 * k, tile]
            second = jnp.where(2 * k + 1 < used, pair_tiles[2 * k + 1, tile], FRAME)
            units[base + k] = tile * 65536 + first * 256 + second
        return base + (used + 1) // 2

    total = lax.fori_loop(0, OWN, list_step, 0)
    for k in range(UNITS):
        units[total + k] = OWN * 65536 + FRAME * 256 + FRAME
    trips[0] = (total + UNITS - 1) // UNITS

    for k in range(9):
        counts[k] = 0
        for m in range(HAND):
            slots[k * OWN + m] = 0
    me = lax.axis_index("dom")

    def slot_step(tile, carry):
        shift = dest[tile] - me
        k = jnp.where(shift == 0, 8, jnp.where(shift < 0, shift + 4, shift + 3))
        n = counts[k]
        slots[k * OWN + n] = tile
        counts[k] = n + 1
        return carry

    lax.fori_loop(0, OWN, slot_step, 0)

    def trip(step, carry):
        for k in range(UNITS):
            unit = units[step * UNITS + k]
            tile, first, second = unit >> 16, (unit >> 8) & 255, unit & 255
            pair = jnp.concatenate([near[first], near[second]], axis=1)
            s = jnp.dot(own[tile], pair, preferred_element_type=F32)
            r = jnp.maximum(s, 0.0)
            square = r * r
            cube = square * r
            fourth = square * square
            acc[0, tile] += (
                cube[:, :WIDE] * chis[pl.ds(first, 1), :] + cube[:, WIDE:] * chis[pl.ds(second, 1), :]
            )
            acc[1, tile] += fourth[:, :WIDE] + fourth[:, WIDE:]
        return carry

    lax.fori_loop(0, trips[0], trip, 0)

    for tile in range(OWN):
        slope[pl.ds(tile, 1), :] = total_rows(acc[0, tile])
        energy[pl.ds(tile, 1), :] = total_rows(acc[1, tile])
    for group in range(OWN // 8):
        rows = pl.ds(group * 8, 8)
        x, y, z, filled, chi = fields(group, pack, ghost)
        root = jnp.sqrt(1.0 + (slope[rows, :] - filled * chi))
        energy[rows, :] = filled * (0.025 * (energy[rows, :] - filled) - embed[rows, :] * root)
        slope[rows, :] = -0.5 * embed[rows, :] * filled / root


def slopes_kernel(
    slope, slist, counts, ghost_slope, ghost_count,
    send, land, send_count, land_count, send_sem, recv_sem, send_sem2, recv_sem2,
):
    barrier = greet()
    for place in range(8):
        for slot in range(8):
            send[place, pl.ds(slot, 1), :] = slope[pl.ds(slist[0, place, slot], 1), :]
        send_count[place] = jnp.full((8, WIDE), counts[place], I32)
    pl.semaphore_wait(barrier, len(OFFSETS))
    copies = []
    for p, shift in enumerate(OFFSETS):
        copies.append(
            send_block(send.at[p], land.at[p], send_sem.at[p], recv_sem.at[p], -shift)
        )
        copies.append(
            send_block(
                send_count.at[p], land_count.at[7 - p], send_sem2.at[p], recv_sem2.at[7 - p], shift
            )
        )
    for p, copy in enumerate(copies):
        copy.wait_send()
    for p, shift in enumerate(OFFSETS):
        copies[2 * p].wait_recv()
        copies[2 * p + 1].wait_recv()
    for place in range(8):
        ghost_slope[pl.ds(place * 8, 8), :] = land[place]
        ghost_count[pl.ds(place, 1), :] = land_count[place, pl.ds(0, 1), :]


def force_kernel(
    pack, ghost, slope, ghost_slope, near, units, trips, slots, counts, ghost_count,
    force, fresh, source,
    own_raw, near_raw, own, near_more, places, acc,
):
    pack = pack.reshape(OWN * 8, WIDE)
    fresh = fresh.reshape(OWN * 8, WIDE)
    zero = jnp.zeros((8, WIDE), F32)
    one = jnp.ones((8, WIDE), F32)
    for group in range(FRAME // 8):
        high, low, whole, norm, filled, chi = place_factors(group, pack, ghost)
        mine = group < OWN // 8
        slopes = slope[pl.ds(group * 8, 8), :] if mine else ghost_slope[pl.ds(group * 8 - OWN, 8), :]
        chi_high, chi_low = two_parts(15.0 * chi)
        slope_high, slope_low = two_parts(15.0 * slopes)
        extra = [chi_high, chi_low, chi_high, slope_high, slope_low, slope_high]
        put_rows(near_raw, group, [one, one] + extra)
        for axis in range(3):
            places[axis, pl.ds(group * 8, 8), :] = 2.0 * whole[axis]
        if mine:
            chi_high, chi_low = two_parts(chi)
            slope_high, slope_low = two_parts(slopes)
            extra = [slope_high, slope_high, slope_low, chi_high, chi_high, chi_low]
            put_rows(own_raw, group, own_rows(high, low, norm) + extra)
    for axis in range(3):
        places[axis, pl.ds(FRAME, 8), :] = zero
    near_more[FRAME] = jnp.zeros((16, WIDE), BF16)

    def near_step(tile, carry):
        rows = near_raw[pl.ds(pl.multiple_of(tile * 8, 8), 8), :]
        near_more[tile] = jnp.concatenate([rows, zero], axis=0).astype(BF16)
        return carry

    lax.fori_loop(0, FRAME, near_step, 0, unroll=8)

    def own_step(tile, carry):
        own[tile] = padded(own_raw, tile).T.astype(BF16)
        for k in range(4):
            acc[k, tile] = jnp.zeros((WIDE, WIDE), F32)
        return carry

    lax.fori_loop(0, OWN, own_step, 0, unroll=4)
    own[OWN] = jnp.zeros((WIDE, FEAT), BF16)

    end = 0
    for k in range(9):
        k = (0, 1, 2, 3, 8, 4, 5, 6, 7)[k]
        for m in range(OWN if k == 8 else HAND):
            source[end + m] = 8 * HAND + slots[8 * OWN + m] if k == 8 else k * HAND + m
        end += counts[8] if k == 8 else ghost_count[k, 0]

    def rest(slot, carry):
        source[slot] = 8 * HAND + OWN
        return carry

    lax.fori_loop(end, CAP, rest, 0)

    def both(tile):
        more = jnp.concatenate([near[tile, pl.ds(0, 16), :], near_more[tile]], axis=0)
        return jnp.concatenate([near[tile], more], axis=1)

    def trip(step, carry):
        for k in range(UNITS):
            unit = units[step * UNITS + k]
            tile, first, second = unit >> 16, (unit >> 8) & 255, unit & 255
            pair = jnp.concatenate([both(first), both(second)], axis=1)
            s = jnp.dot(own[tile], pair, preferred_element_type=F32)
            r1 = jnp.maximum(s[:, 0:WIDE], 0.0)
            r2 = jnp.maximum(s[:, 2 * WIDE : 3 * WIDE], 0.0)
            c1 = r1 * r1 * s[:, WIDE : 2 * WIDE]
            c2 = r2 * r2 * s[:, 3 * WIDE : 4 * WIDE]
            acc[0, tile] += c1 + c2
            for axis in range(3):
                acc[1 + axis, tile] += (
                    c1 * places[axis, pl.ds(first, 1), :] + c2 * places[axis, pl.ds(second, 1), :]
                )
        return carry

    lax.fori_loop(0, trips[0], trip, 0)

    for tile in range(OWN):
        for k in range(4):
            own_raw[pl.ds(k * OWN + tile, 1), :] = total_rows(acc[k, tile])
    for group in range(OWN // 8):
        filled = pack[every(group * 64 + 6, 8), :]
        for axis in range(3):
            rows = pl.ds(group * 8, 8)
            place = places[axis, rows, :]
            pulled = own_raw[pl.ds((1 + axis) * OWN + group * 8, 8), :]
            push = (place * own_raw[rows, :] - pulled) * (0.1 * filled)
            speed = pack[every(group * 64 + 3 + axis, 8), :] + STEP * push
            fresh[every(group * 64 + axis, 8), :] = pack[every(group * 64 + axis, 8), :] + STEP * speed
            fresh[every(group * 64 + 3 + axis, 8), :] = speed
            near_raw[every(group * 64 + axis, 8), :] = push
        fresh[every(group * 64 + 6, 8), :] = filled
        fresh[every(group * 64 + 7, 8), :] = zero
    for tile in range(OWN):
        force[:, pl.ds(tile * WIDE, WIDE)] = near_raw[pl.ds(tile * 8, 3), :]


def moving_kernel(fresh, slots, pool, send, land, send_sem, recv_sem):
    barrier = greet()
    for place in range(8):
        for m in range(HAND):
            send[place, m] = fresh[slots[place * OWN + m]]
    pl.semaphore_wait(barrier, len(OFFSETS))
    copies = [
        send_block(send.at[p], land.at[7 - p], send_sem.at[p], recv_sem.at[7 - p], shift)
        for p, shift in enumerate(OFFSETS)
    ]
    for tile in range(OWN):
        pool[8 * HAND + tile] = fresh[tile]
    pool[8 * HAND + OWN] = jnp.zeros((8, WIDE), F32)
    for copy in copies:
        copy.wait()
    for place in range(8):
        for m in range(HAND):
            pool[place * HAND + m] = land[place, m]


def placing_kernel(pool, source, moved, count):
    total = jnp.zeros((8, WIDE), F32)
    for slot in range(CAP):
        held = pool[source[slot]]
        total = total + held
        moved[:, pl.ds(slot * WIDE, WIDE)] = held[0:7]
    count[0] = jnp.sum(total[6:7]).astype(I32)


def on(space):
    return pl.BlockSpec(memory_space=space)


def call(kernel, name, ins, outs, scratch, collective=None):
    return pl.pallas_call(
        kernel,
        name=name,
        in_specs=[on(space) for space in ins],
        out_shape=outs,
        out_specs=[on(SMEM if out.dtype == I32 and len(out.shape) == 1 else VMEM) for out in outs],
        scratch_shapes=scratch,
        compiler_params=pltpu.CompilerParams(collective_id=collective, has_side_effects=True),
    )


def plain(*dims, dtype=F32):
    return jax.ShapeDtypeStruct(dims, dtype)


def kept(*dims, dtype=F32):
    return KEPT(dims, dtype)


def near_by(value):
    return pltpu.with_memory_space_constraint(value, VMEM)


def per_device(
    positions,
    velocity,
    density_weight,
    embed_strength,
    occupied,
    send_list,
    send_count,
    pair_tiles,
    pair_count,
    migrate_dest,
):
    dma = pltpu.SemaphoreType.DMA
    chi = density_weight.reshape(OWN, WIDE)
    embed = embed_strength.reshape(OWN, WIDE)
    occ = occupied.reshape(OWN, WIDE)
    pack, ghost = call(
        atoms_kernel,
        "atoms",
        [VMEM] * 4 + [SMEM, VMEM],
        [kept(OWN, 8, WIDE), kept(8, 40, WIDE)],
        [VMEM((8, 40, WIDE), F32), VMEM((8, 40, WIDE), F32), dma((8,)), dma((8,))],
        0,
    )(positions, velocity, chi, occ, send_list, send_count)
    slope, energy, near, units, trips, slots, counts = call(
        density_kernel,
        "density",
        [VMEM] * 3 + [SMEM] * 3,
        [
            kept(OWN, WIDE),
            plain(OWN, WIDE),
            kept(FRAME + 1, FEAT, WIDE, dtype=BF16),
            plain(LIST, dtype=I32),
            plain(1, dtype=I32),
            plain(9 * OWN, dtype=I32),
            plain(9, dtype=I32),
        ],
        [
            VMEM((OWN * ROWS, WIDE), F32),
            VMEM((FRAME * ROWS, WIDE), F32),
            VMEM((OWN + 1, WIDE, FEAT), BF16),
            VMEM((FRAME + 8, WIDE), F32),
            VMEM((2, OWN + 1, WIDE, WIDE), F32),
        ],
    )(near_by(pack), near_by(ghost), embed, pair_tiles.T, pair_count, migrate_dest)
    ghost_slope, ghost_count = call(
        slopes_kernel,
        "slopes",
        [VMEM, SMEM, SMEM],
        [kept(GHOST, WIDE), plain(8, WIDE, dtype=I32)],
        [
            VMEM((8, 8, WIDE), F32),
            VMEM((8, 8, WIDE), F32),
            VMEM((8, 8, WIDE), I32),
            VMEM((8, 8, WIDE), I32),
        ]
        + [dma((8,))] * 4,
        1,
    )(near_by(slope), send_list, counts)
    force, fresh, source = call(
        force_kernel,
        "force",
        [VMEM] * 5 + [SMEM] * 5,
        [plain(3, OWN * WIDE), kept(OWN, 8, WIDE), plain(CAP + OWN + 8, dtype=I32)],
        [
            VMEM((OWN * ROWS, WIDE), F32),
            VMEM((FRAME * 8, WIDE), F32),
            VMEM((OWN + 1, WIDE, FEAT), BF16),
            VMEM((FRAME + 1, 16, WIDE), BF16),
            VMEM((3, FRAME + 8, WIDE), F32),
            VMEM((4, OWN + 1, WIDE, WIDE), F32),
        ],
    )(near_by(pack), near_by(ghost), near_by(slope), near_by(ghost_slope), near_by(near), units, trips, slots, counts, ghost_count)
    (pool,) = call(
        moving_kernel,
        "moving",
        [VMEM, SMEM],
        [kept(8 * HAND + OWN + 1, 8, WIDE)],
        [VMEM((8, HAND, 8, WIDE), F32), VMEM((8, HAND, 8, WIDE), F32), dma((8,)), dma((8,))],
        2,
    )(near_by(fresh), slots)
    moved, moved_count = call(
        placing_kernel,
        "placing",
        [VMEM, SMEM],
        [plain(7, CAP * WIDE), plain(1, dtype=I32)],
        [],
    )(near_by(pool), source)
    return force, energy.reshape(OWN * WIDE), moved, moved_count


def solution(mesh):
    return jax.shard_map(
        per_device,
        mesh=mesh,
        in_specs=(
            P(None, "dom"),
            P(None, "dom"),
            P("dom"),
            P("dom"),
            P("dom"),
            P("dom", None, None),
            P("dom", None),
            P("dom", None),
            P("dom"),
            P("dom"),
        ),
        out_specs=(P(None, "dom"), P("dom"), P(None, "dom"), P("dom")),
        check_vma=False,
    )
```

time: 422 us -> 75.2 us (0.18)
  the two profiles are of different devices: /device:TPU:2 before, /device:TPU:1 now
where the time goes in v1:
time: 75.2 us; the launch traced here: 74.1 us
  Pallas kernels  73.4 us (98%)
    pallas_call x1, Pallas kernels, per_device(): call(force_kernel, 'force', [VMEM] * 5 + [SMEM] * 5, [plain(3, OWN * WIDE...  18.6 us
    pallas_call x1, Pallas kernels, per_device(): call(density_kernel, 'density', [VMEM] * 3 + [SMEM] * 3, [kept(OWN, WIDE)...  15.8 us
    pallas_call x1, Pallas kernels, per_device(): call(atoms_kernel, 'atoms', [VMEM] * 4 + [SMEM, VMEM], [kept(OWN, 8, WIDE...  13.8 us
    pallas_call x1, Pallas kernels, per_device(): call(slopes_kernel, 'slopes', [VMEM, SMEM, SMEM], [kept(GHOST, WIDE), pla...  12.1 us
    pallas_call x1, Pallas kernels, per_device(): call(moving_kernel, 'moving', [VMEM, SMEM], [kept(8 * HAND + OWN + 1, 8,...  11.6 us

profile of v1, /device:TPU:1, one launch (start us, length us, event | category | flops | bytes accessed | tf_op | source)
XLA Modules:
  0.0 74.1 jit_solution(4993717391168382509)
XLA Ops:
  0.6 13.8 %atoms.1 = (f32[32,8,128]{2,1,0:T(8,128)S(1)}, f32[8,40,128]{2,1,0:T(8,128)S(1)}) custom-call(f32[3,4096]{1,0:T(4,128)} %pos.1, f32[3,4096]{1,0:T(4,128)} %vel.1, f32[32,128]{1,0:T(8,128)} %bitcast.6, s32[32,128]{1,0:T(8,128)} %bitcast.7, s32[1,8,8]{2,1,0:T(8,128)} %slist.3, s32[1,8]{1,0:T(1,128)} %scount.1), custom_call_target="tpu_custom_call" | custom-call | tf_op jit(solution)/shard_map/atoms/pallas_call | solution.py:449
  14.5 15.8 %density.1 = (f32[32,128]{1,0:T(8,128)S(1)}, f32[32,128]{1,0:T(8,128)}, bf16[97,32,128]{2,1,0:T(8,128)(2,1)S(1)}, s32[412]{0:T(512)}, s32[1]{0:T(128)}, /*index=5*/s32[288]{0:T(512)}, s32[9]{0:T(128)}) custom-call(f32[32,8,128]{2,1,0:T(8,128)S(1)} %get-tuple-element.20.pack, f32[8,40,128]{2,1,0:T(8,128)S(1)} %get-tuple-element.21.ghost, f32[32,128]{1,0:T(8,128)} %bitcast.5, ...), custom_call_target="tpu_custom_call" | custom-call | tf_op jit(solution)/shard_map/density/pallas_call | solution.py:457
  30.3 12.1 %slopes.1 = (f32[64,128]{1,0:T(8,128)S(1)}, s32[8,128]{1,0:T(8,128)}) custom-call(f32[32,128]{1,0:T(8,128)S(1)} %get-tuple-element.22.slope, s32[1,8,8]{2,1,0:T(8,128)} %slist.3, s32[9]{0:T(128)} %get-tuple-element.23.counts), custom_call_target="tpu_custom_call" | custom-call | tf_op jit(solution)/shard_map/slopes/pallas_call | solution.py:478
  42.5 18.6 %force.1 = (f32[3,4096]{1,0:T(4,128)}, f32[32,8,128]{2,1,0:T(8,128)S(1)}, s32[104]{0:T(128)}) custom-call(f32[32,8,128]{2,1,0:T(8,128)S(1)} %get-tuple-element.20.pack, f32[8,40,128]{2,1,0:T(8,128)S(1)} %get-tuple-element.21.ghost, f32[32,128]{1,0:T(8,128)S(1)} %get-tuple-element.22.slope, f32[64,128]{1,0:T(8,128)S(1)} %get-tuple-element.24.ghost_slope, ...), custom_call_target="tpu_custom_call" | custom-call | tf_op jit(solution)/shard_map/force/pallas_call | solution.py:492
  61.1 11.6 %moving.1.pool = f32[65,8,128]{2,1,0:T(8,128)S(1)} custom-call(f32[32,8,128]{2,1,0:T(8,128)S(1)} %get-tuple-element.32.fresh, s32[288]{0:T(512)} %get-tuple-element.28.slots), custom_call_target="tpu_custom_call" | custom-call | tf_op jit(solution)/shard_map/moving/pallas_call | solution.py:506
  72.6 1.4 %placing.1 = (f32[7,8192]{1,0:T(8,128)}, s32[1]{0:T(128)}) custom-call(f32[65,8,128]{2,1,0:T(8,128)S(1)} %moving.1.pool, s32[104]{0:T(128)} %get-tuple-element.33.source), custom_call_target="tpu_custom_call" | custom-call | tf_op jit(solution)/shard_map/placing/pallas_call | solution.py:514
